TPU v7x, 32 devices: a whole 2x2x4 slice. The times are simulated.
32 devices in a mesh: lon: 4 (over y, x), lat: 4 (over z), mem: 2 (over core).
Axes of the slice: x: 2, y: 2, z: 4, core: 2. Of those that a mesh axis runs over, the one named last changes fastest.
Arguments:
- north_vel: bfloat16 [2, 4, 75, 128, 512], P('mem', None, None, 'lat', 'lon'), may hold values from -6 to 6
- up_vel: bfloat16 [2, 4, 75, 128, 512], P('mem', None, None, 'lat', 'lon'), may hold values from -6 to 6
- dens_class: int32 [2, 4, 75, 128, 512], P('mem', None, None, 'lat', 'lon'), may hold values from 0 to 79
- thickness: int32 [75, 128, 512], P(None, 'lat', 'lon'), may hold values from 0 to 2000
- basin_id: int32 [128, 512], P('lat', 'lon'), may hold values from 0 to 3
Outputs:
- depth_mean: float32 [4, 4, 2, 75, 128], P('lon', None, None, None, 'lat')
- depth_spread: float32 [4, 4, 2, 75, 128], P('lon', None, None, None, 'lat')
- class_mean: float32 [4, 4, 2, 80, 128], P('lon', None, None, None, 'lat')
- class_spread: float32 [4, 4, 2, 80, 128], P('lon', None, None, None, 'lat')
Inputs may be any that keep to these rules, and one draw needn't show every extreme that they name: `basin_id`: 0 marks land; 1 to 3 name the basins. `thickness`: thousandths of a unit layer; 0 marks a cell below the sea floor.
All inputs are finite; a program needn't handle non-finite values.
Results may differ from a plain program's by a relative error of at most 0.0029.
Values sent between devices are 32-bit elements; how exact they have to be, the bound alone decides.
A program may use at most 128 MiB of HBM per device.

v0:
```python
import math

import jax
import jax.numpy as jnp
from jax import lax
from jax.experimental import pallas as pl
from jax.experimental.pallas import tpu as pltpu
from jax.sharding import PartitionSpec as P

CLASSES = 80
BASINS = 3
REGIONS = BASINS + 1
LOW = 32
SUB = 8


north_unit = 0.02
up_unit = 0.01

F32, BF16, F8 = jnp.float32, jnp.bfloat16, jnp.float8_e4m3fn
NT = (((1,), (1,)), ((), ()))
NN = (((1,), (0,)), ((), ()))


def round_up(n, k):
    return -(-n // k) * k


def iota(shape, axis):
    return lax.broadcasted_iota(jnp.int32, shape, axis)


def split(x):
    high = x.astype(BF16)
    return high, (x - high.astype(F32)).astype(BF16)


def exact_dot(ones, x, dims, ones_first=True):
    high, low = split(x)
    if ones_first:
        return lax.dot_general(ones, high, dims, preferred_element_type=F32) + lax.dot_general(
            ones, low, dims, preferred_element_type=F32
        )
    return lax.dot_general(high, ones, dims, preferred_element_type=F32) + lax.dot_general(
        low, ones, dims, preferred_element_type=F32
    )


def sizes_of(levels, rows):
    return dict(
        levels=levels,
        rows=rows,
        highs=-(-BASINS * CLASSES // LOW),
        span=-(-CLASSES // LOW),
        deep=round_up(levels, 16),
        even=round_up(levels, 2),
        lanes=REGIONS * rows,
    )


def first_high(b):
    return b * CLASSES // LOW


def prepare(sz, basin, consts):
    base_ref, mask_ref, upto_class, upto_level, upto_row = consts
    rows, lanes = sz["rows"], sz["lanes"]
    lons = basin.shape[1]
    base_ref[...] = jnp.where(basin > 0, (basin - 1) * CLASSES, -LOW * 64)
    regions = [basin > 0] + [basin == r for r in range(1, REGIONS)]
    mask = jnp.concatenate([jnp.where(r, 1.0, 0.0) for r in regions], axis=0)
    group = iota((lanes, lons), 0) % rows // SUB
    mask_ref[...] = jnp.concatenate(
        [jnp.where(group == g, mask, 0.0) for g in range(rows // SUB)], axis=1
    ).astype(BF16)

    shape = upto_class.shape[1:]
    item = iota(shape, 1) // SUB
    part, half = item % LOW // 2, item % 2
    target = jnp.where(half == 0, part, jnp.where(part == 0, LOW // 2, LOW - part))
    sign = jnp.where((half == 1) & (part > 0), -1.0, 1.0)
    count = (half == 0) & (part == 0)

    def weight(m):
        beyond = jnp.where(count & (m > LOW // 2) & (m < LOW), 1.0, 0.0)
        return jnp.where(m == target, sign, 0.0) + beyond

    for b in range(BASINS):
        low = b * CLASSES - (first_high(b) + item // LOW) * LOW
        start, stop = jnp.maximum(low, 0), jnp.minimum(low + iota(shape, 0), LOW - 1) + 1
        upto_class[b] = jnp.where(stop > start, weight(start) - weight(stop), 0.0).astype(BF16)
    shape = upto_level.shape
    upto_level[...] = jnp.where(iota(shape, 1) <= iota(shape, 0), 1.0, 0.0).astype(BF16)
    shape = upto_row.shape
    a, b = iota(shape, 0), iota(shape, 1)
    upto_row[...] = jnp.where((a // rows == b // rows) & (a <= b), 1.0, 0.0).astype(BF16)


def month_tables(sz, north, up, dens, thick, coef, consts, work, put):
    base_ref, mask_ref, upto_class, upto_level, upto_row = consts
    flux, depth, step_high, step_low = work
    rows, highs, levels, lanes = sz["rows"], sz["highs"], sz["levels"], sz["lanes"]
    groups, even, span = rows // SUB, sz["even"], sz["span"]
    zero = jnp.zeros((2 * SUB, 128), BF16)
    width = LOW * SUB

    upper = iota((2 * SUB, 128), 0) >= SUB
    lane = iota((SUB, width), 1)
    own = iota((SUB, width), 0) == lane % SUB
    inner = lane >= 4 * SUB

    for pair in range(rows // (2 * SUB)):
        cells = slice(pair * 2 * SUB, (pair + 1) * 2 * SUB)
        lhs, rhs = ([], []), ([], [])
        kept = None
        for k in range(levels):
            depth_k = thick[k, cells, :].astype(F32)
            nf = north[k, cells, :].astype(F32) * (coef[0, cells, :] * depth_k)
            rf = up[k, cells, :].astype(F32) * (coef[1, cells, :] * jnp.minimum(depth_k, 1.0))
            if k % 2 == 1 or k == levels - 1:
                first = kept if k % 2 == 1 else (nf, rf)
                second = (nf, rf) if k % 2 == 1 else (jnp.zeros_like(nf),) * 2
                for s in range(2):
                    for half in range(2):
                        part = slice(half * SUB, (half + 1) * SUB)
                        flux[s, 2 * pair + half, pl.ds(k // 2 * 2 * SUB, 2 * SUB), :] = (
                            jnp.concatenate([first[s][part], second[s][part]], 0).astype(BF16)
                        )
            kept = (nf, rf)
            q = base_ref[cells, :] + dens[k, cells, :]
            qf, lo = q.astype(F32), (q & (LOW - 1)).astype(F32)
            for half in range(2):
                part = slice(half * SUB, (half + 1) * SUB)
                join = lambda x, y: jnp.concatenate([x[part], y[part]], 0).astype(BF16)
                at_least = join(qf, qf - LOW)
                ends = join(lo, (LOW - 1) - lo)
                top = jnp.where(join(jnp.full_like(lo, LOW), lo) >= BF16(LOW // 2), BF16(1), zero)
                parts = [top] + [jnp.minimum(ends, BF16(p)) for p in range(1, LOW // 2)]
                rhs[half].append(jnp.concatenate(parts, 0).astype(F8))
                hits = [at_least >= BF16(2 * LOW * p) for p in range(highs // 2)]
                nd, rd = join(nf, nf), join(rf, rf)
                lhs[half].append(
                    jnp.concatenate(
                        [jnp.where(h, nd, zero) for h in hits]
                        + [jnp.where(h, rd, zero) for h in hits],
                        0,
                    )
                )
        for half in range(2):
            sums = lax.dot_general(
                jnp.concatenate(lhs[half], 1),
                jnp.concatenate(rhs[half], 1),
                NT,
                preferred_element_type=F32,
            )
            for s in range(2):
                for h in range(highs):
                    at = (s * highs + h) * SUB
                    here = sums[at : at + SUB]
                    if h + 1 < highs:
                        here = here - sums[at + SUB : at + 2 * SUB]
                    here = jnp.where(own, here, 0.0)
                    back = jnp.concatenate(
                        [pltpu.roll(here[:, c : c + 128], 2 * SUB, 1) for c in range(0, width, 128)],
                        1,
                    )
                    first = back[:, :128]
                    turned = [jnp.where(inner[:, :128], first, 0.0)]
                    for c in range(128, width, 128):
                        turned.append(
                            jnp.where(
                                lane[:, :128] < 2 * SUB, back[:, c - 128 : c], back[:, c : c + 128]
                            )
                        )
                    here = here - jnp.concatenate(turned, 1)
                    row = (s * groups + 2 * pair + half) * SUB
                    high, low = split(here)
                    step_high[row : row + SUB, h * width : (h + 1) * width] = high
                    step_low[row : row + SUB, h * width : (h + 1) * width] = low

    found = []
    for b in range(BASINS):
        cols = slice(first_high(b) * width, (first_high(b) + span) * width)
        found.append(
            lax.dot_general(upto_class[b], step_high[:, cols], NT, preferred_element_type=F32)
            + lax.dot_general(upto_class[b], step_low[:, cols], NT, preferred_element_type=F32)
        )
    found = [sum(found[1:], found[0])] + found
    row_own = iota((SUB, lanes), 0) == iota((SUB, lanes), 1) % SUB
    for s in range(2):
        total = jnp.concatenate([x[:, s * rows : (s + 1) * rows] for x in found], 1)
        cols = jnp.concatenate([flux[s, g] for g in range(groups)], 1)
        seen = lax.dot_general(cols, mask_ref[...], NT, preferred_element_type=F32)
        seen = jnp.where(row_own[None], seen.reshape(even, SUB, lanes), 0.0)
        depth[0:even, :] = jnp.sum(seen, axis=1)
        if s == 0:
            put(0, total)
            put(2, exact_dot(upto_level[...], depth[...], NN))
        else:
            put(1, exact_dot(upto_row[...], total, NN, False))
            put(3, exact_dot(upto_row[...], depth[...], NN, False))


def table_rows(sz):
    return [0, CLASSES, 2 * CLASSES, 2 * CLASSES + sz["deep"], 2 * (CLASSES + sz["deep"])]


def const_shapes(sz, lons):
    rows, lanes = sz["rows"], sz["lanes"]
    return [
        pltpu.VMEM((rows, lons), jnp.int32),
        pltpu.VMEM((lanes, rows // SUB * lons), BF16),
        pltpu.VMEM((BASINS, CLASSES, sz["span"] * LOW * SUB), BF16),
        pltpu.VMEM((sz["deep"], sz["deep"]), BF16),
        pltpu.VMEM((lanes, lanes), BF16),
    ]


def work_shapes(sz, lons):
    rows = sz["rows"]
    steps = pltpu.VMEM((2 * rows, sz["highs"] * LOW * SUB), BF16)
    return [
        pltpu.VMEM((2, rows // SUB, sz["even"] * SUB, lons), BF16),
        pltpu.VMEM((sz["deep"], sz["lanes"]), F32),
        steps,
        steps,
    ]


def fused(sz, north_vel, up_vel, dens_class, thickness, basin_id):
    _, months, levels, rows, lons = north_vel.shape
    lanes, deep = sz["lanes"], sz["deep"]
    at = table_rows(sz)
    tall = at[-1]
    ends = CLASSES + deep
    devices, lats, members = (lax.axis_size(a) for a in ("lon", "lat", "mem"))
    assert months == devices
    far = [(de, dl) for dl in range(1, lats) for de in range(members)]

    def kernel(north_h, up_h, dens_h, thick_h, basin_h, final, *scratch):
        consts, work, rest = scratch[:5], scratch[5:9], scratch[9:]
        (north, up, dens, thick, basin, coef, tab, inbox, mine, membox, tail, tailbox) = rest[:12]
        in_sem, fix_sem, send, recv, msend, mrecv, tsend, trecv = rest[12:]
        me, lat, mem = (lax.axis_index(a) for a in ("lon", "lat", "mem"))

        def inputs(t):
            month = lax.rem(me + 1 + t, devices)
            return [
                pltpu.make_async_copy(h.at[0, month], v.at[t], in_sem.at[t, i])
                for i, (h, v) in enumerate(((north_h, north), (up_h, up), (dens_h, dens)))
            ]

        fixed = [
            pltpu.make_async_copy(basin_h, basin, fix_sem.at[0]),
            pltpu.make_async_copy(thick_h, thick, fix_sem.at[1]),
        ]
        for copy in fixed + inputs(0):
            copy.start()
        for t in range(1, devices):
            for copy in inputs(t):
                copy.start()

        barrier = pltpu.get_barrier_semaphore()
        peers = [{"lon": lax.rem(me + d, devices)} for d in range(1, devices)]
        peers += [
            {"lat": lax.rem(lat + dl, lats), "mem": lax.rem(mem + de, members)}
            for dl in range(lats)
            for de in range(members)
            if dl or de
        ]
        for peer in peers:
            pl.semaphore_signal(
                barrier, inc=1, device_id=peer, device_id_type=pl.DeviceIdType.MESH
            )

        index = lat * rows + iota((rows, lons), 0)
        latitude = (-78.0 + 156.0 * (index.astype(F32) + 0.5) / (rows * lats)) * (math.pi / 180.0)
        width = jnp.cos(latitude)
        coef[0] = (north_unit * 0.001) * width
        coef[1] = up_unit * width
        work[1][...] = jnp.zeros_like(work[1])
        fixed[0].wait()
        prepare(sz, basin[...], consts)
        fixed[1].wait()

        def table_copy(t):
            return pltpu.make_async_remote_copy(
                src_ref=tab.at[t],
                dst_ref=inbox.at[t],
                send_sem=send.at[t],
                recv_sem=recv.at[t],
                device_id={"lon": lax.rem(me + 1 + t, devices)},
                device_id_type=pl.DeviceIdType.MESH,
            )

        def one_month(t, carry):
            for copy in inputs(t):
                copy.wait()

            def put(i, x):
                tab[t, at[i] : at[i + 1], :] = x

            month_tables(
                sz, north.at[t], up.at[t], dens.at[t], thick, coef, consts, work, put
            )

            @pl.when(t == 0)
            def _():
                pl.semaphore_wait(barrier, len(peers))

            @pl.when(t < devices - 1)
            def _():
                table_copy(t).start()

            return carry

        lax.fori_loop(0, devices, one_month, 0)

        total = tab[devices - 1]
        for t in range(devices - 1):
            table_copy(t).wait_recv()
            total = total + inbox[t]
        mine[...] = total
        copies = [
            pltpu.make_async_remote_copy(
                src_ref=mine,
                dst_ref=membox.at[de - 1],
                send_sem=msend.at[de - 1],
                recv_sem=mrecv.at[de - 1],
                device_id={"mem": lax.rem(mem + de, members)},
                device_id_type=pl.DeviceIdType.MESH,
            )
            for de in range(1, members)
        ]
        for copy in copies:
            copy.start()

        pick = (iota((2 * SUB, lanes), 1) == iota((2 * SUB, lanes), 0) * rows + rows - 1)
        pick = jnp.where(pick, 1.0, 0.0).astype(BF16)
        rise = jnp.concatenate([mine[at[1] : at[2], :], mine[at[3] : at[4], :]], 0)
        high, low = split(rise)
        tail[...] = lax.dot_general(pick, high, NT, preferred_element_type=F32) + lax.dot_general(
            pick, low, NT, preferred_element_type=F32
        )
        tails = [
            pltpu.make_async_remote_copy(
                src_ref=tail,
                dst_ref=tailbox.at[i],
                send_sem=tsend.at[i],
                recv_sem=trecv.at[i],
                device_id={"lat": lax.rem(lat + dl, lats), "mem": lax.rem(mem + de, members)},
                device_id_type=pl.DeviceIdType.MESH,
            )
            for i, (de, dl) in enumerate(far)
        ]
        for copy in tails:
            copy.start()

        wide = (iota((2 * SUB, lanes), 1) // rows) == iota((2 * SUB, lanes), 0)
        wide = jnp.where(wide, 1.0, 0.0).astype(BF16)
        for copy in tails:
            copy.wait_recv()
        for copy in copies:
            copy.wait_recv()
        for de in range(members):
            whole = mine if de == 0 else membox.at[de - 1]
            south = jnp.zeros((2 * SUB, ends), F32)
            for i, (other, dl) in enumerate(far):
                if other == de:
                    south = south + jnp.where(lat >= dl, tailbox[i], 0.0)
            high, low = split(south)
            tn = (((0,), (0,)), ((), ()))
            carry = lax.dot_general(
                high, wide, tn, preferred_element_type=F32
            ) + lax.dot_general(low, wide, tn, preferred_element_type=F32)
            final[de, at[0] : at[1], :] = whole[at[0] : at[1], :]
            final[de, at[1] : at[2], :] = whole[at[1] : at[2], :] + carry[:CLASSES]
            final[de, at[2] : at[3], :] = whole[at[2] : at[3], :]
            final[de, at[3] : at[4], :] = whole[at[3] : at[4], :] + carry[CLASSES:]

        for t in range(devices - 1):
            table_copy(t).wait_send()
        for copy in copies + tails:
            copy.wait_send()

    slots = max(1, devices - 1)
    dma = pltpu.SemaphoreType.DMA
    return pl.pallas_call(
        kernel,
        out_shape=jax.ShapeDtypeStruct((members, tall, lanes), F32),
        in_specs=[pl.BlockSpec(memory_space=pl.ANY)] * 5,
        out_specs=pl.BlockSpec(memory_space=pltpu.VMEM),
        scratch_shapes=const_shapes(sz, lons)
        + work_shapes(sz, lons)
        + [
            pltpu.VMEM((months, levels, rows, lons), north_vel.dtype),
            pltpu.VMEM((months, levels, rows, lons), up_vel.dtype),
            pltpu.VMEM((months, levels, rows, lons), dens_class.dtype),
            pltpu.VMEM((levels, rows, lons), thickness.dtype),
            pltpu.VMEM((rows, lons), basin_id.dtype),
            pltpu.VMEM((2, rows, lons), F32),
            pltpu.VMEM((devices, tall, lanes), F32),
            pltpu.VMEM((slots, tall, lanes), F32),
            pltpu.VMEM((tall, lanes), F32),
            pltpu.VMEM((members - 1, tall, lanes), F32),
            pltpu.VMEM((2 * SUB, ends), F32),
            pltpu.VMEM((len(far), 2 * SUB, ends), F32),
            dma((devices, 3)),
            dma((2,)),
            dma((slots,)),
            dma((slots,)),
            dma((members - 1,)),
            dma((members - 1,)),
            dma((len(far),)),
            dma((len(far),)),
        ],
        compiler_params=pltpu.CompilerParams(
            collective_id=0, has_side_effects=True, vmem_limit_bytes=60 * 2**20
        ),
    )(north_vel, up_vel, dens_class, thickness, basin_id)


def moments(sz, final):
    members = final.shape[0]
    at, rows, levels, lanes = table_rows(sz), sz["rows"], sz["levels"], sz["lanes"]

    def kernel(final, o_dm, o_ds, o_cm, o_cs):
        for s in range(2):
            for i, count, o_mean, o_spread in ((s, CLASSES, o_cm, o_cs), (2 + s, levels, o_dm, o_ds)):
                part = [final[de, at[i] : at[i + 1], :] for de in range(members)]
                mean = sum(part[1:], part[0]) / members
                square = [jnp.square(x - mean) for x in part]
                spread = jnp.sqrt(sum(square[1:], square[0]) / (members - 1))
                for o, x in ((o_mean, mean), (o_spread, spread)):
                    pad = round_up(x.shape[0], 128) - x.shape[0]
                    x = jnp.concatenate([x, jnp.zeros((pad, lanes), F32)], 0).T
                    for r in range(REGIONS):
                        o[0, r, s] = x[r * rows : (r + 1) * rows, :count]

    out = lambda n: jax.ShapeDtypeStruct((1, REGIONS, 2, rows, n), F32)
    outs = pl.pallas_call(
        kernel,
        out_shape=[out(levels), out(levels), out(CLASSES), out(CLASSES)],
        in_specs=[pl.BlockSpec(memory_space=pltpu.VMEM)],
        out_specs=[pl.BlockSpec(memory_space=pltpu.VMEM)] * 4,
    )(final)
    return tuple(jnp.swapaxes(x, 3, 4) for x in outs)


def body(north_vel, up_vel, dens_class, thickness, basin_id):
    levels, rows = north_vel.shape[2:4]
    sz = sizes_of(levels, rows)
    return moments(sz, fused(sz, north_vel, up_vel, dens_class, thickness, basin_id))


def solution(mesh):
    in_specs = (
        P("mem", None, None, "lat", "lon"),
        P("mem", None, None, "lat", "lon"),
        P("mem", None, None, "lat", "lon"),
        P(None, "lat", "lon"),
        P("lat", "lon"),
    )
    out_specs = (P("lon", None, None, None, "lat"),) * 4
    return jax.shard_map(body, mesh=mesh, in_specs=in_specs, out_specs=out_specs, check_vma=False)
```

profile of v0, /device:TPU:0, one launch (start us, length us, event | category | flops | bytes accessed | tf_op | source)
XLA Modules:
  0.0 32.7 jit_solution(12558098890943405937)
XLA Ops:
  0.6 30.1 %shard_map.84.final = f32[2,320,128]{2,1,0:T(8,128)} custom-call(bf16[1,4,75,32,128]{4,3,2,1,0:T(8,128)(2,1)} %north_h.1, bf16[1,4,75,32,128]{4,3,2,1,0:T(8,128)(2,1)} %up_h.1, s32[1,4,75,32,128]{4,3,2,1,0:T(8,128)} %dens_h.1, s32[75,32,128]{2,1,0:T(8,128)} %thick_h.1, s32[32,128]{1,0:T(8,128)} %basin_h.1), custom_call_target="tpu_custom_call" | custom-call | tf_op jit(solution)/shard_map/pallas_call | solution.py:388
  30.7 1.9 %shard_map.85 = (f32[1,4,2,32,75]{4,3,2,1,0:T(8,128)}, f32[1,4,2,32,75]{4,3,2,1,0:T(8,128)}, f32[1,4,2,32,80]{4,3,2,1,0:T(8,128)}, f32[1,4,2,32,80]{4,3,2,1,0:T(8,128)}) custom-call(f32[2,320,128]{2,1,0:T(8,128)} %shard_map.84.final), custom_call_target="tpu_custom_call" | custom-call | tf_op jit(solution)/shard_map/pallas_call | solution.py:441
where the time goes:
time: 32.8 us; the launch traced here: 32.7 us
  Pallas kernels  32 us (98%)
  between operations  0.64 us (2%)
    pallas_call x1, Pallas kernels, fused(): pl.pallas_call(kernel, out_shape=jax.ShapeDtypeStruct((members, tall, lan...  30.1 us
    pallas_call x1, Pallas kernels, moments(): pl.pallas_call(kernel, out_shape=[out(levels), out(levels), out(CLASSES),...  1.95 us

commit v1 on v0

v1 whole, which is shorter than its diff:
```python
import math

import jax
import jax.numpy as jnp
from jax import lax
from jax.experimental import pallas as pl
from jax.experimental.pallas import tpu as pltpu
from jax.sharding import PartitionSpec as P

CLASSES = 80
BASINS = 3
REGIONS = BASINS + 1
LOW = 32
SUB = 8


north_unit = 0.02
up_unit = 0.01

F32, BF16, F8 = jnp.float32, jnp.bfloat16, jnp.float8_e4m3fn
NT = (((1,), (1,)), ((), ()))
NN = (((1,), (0,)), ((), ()))


def round_up(n, k):
    return -(-n // k) * k


def iota(shape, axis):
    return lax.broadcasted_iota(jnp.int32, shape, axis)


def split(x):
    high = x.astype(BF16)
    return high, (x - high.astype(F32)).astype(BF16)


def exact_dot(ones, x, dims, ones_first=True):
    high, low = split(x)
    if ones_first:
        return lax.dot_general(ones, high, dims, preferred_element_type=F32) + lax.dot_general(
            ones, low, dims, preferred_element_type=F32
        )
    return lax.dot_general(high, ones, dims, preferred_element_type=F32) + lax.dot_general(
        low, ones, dims, preferred_element_type=F32
    )


def sizes_of(levels, rows):
    return dict(
        levels=levels,
        rows=rows,
        pairs=rows // (2 * SUB),
        highs=-(-BASINS * CLASSES // LOW),
        span=-(-CLASSES // LOW),
        even=round_up(levels, SUB),
        wide=round_up(max(levels, CLASSES), 128),
        lanes=REGIONS * rows,
    )


def first_high(b):
    return b * CLASSES // LOW


def prepare(sz, basin, consts):
    base_ref, mask_ref, upto_class, upto_level, upto_row = consts
    rows = sz["rows"]
    base_ref[...] = jnp.where(basin > 0, (basin - 1) * CLASSES, -LOW * 64)
    regions = [basin > 0] + [basin == r for r in range(1, REGIONS)]
    regions = [jnp.where(r, 1.0, 0.0) for r in regions]
    item = iota((REGIONS * 2 * SUB, basin.shape[1]), 0) % (2 * SUB) // SUB
    for pair in range(sz["pairs"]):
        cells = slice(pair * 2 * SUB, (pair + 1) * 2 * SUB)
        mask = jnp.concatenate([r[cells] for r in regions], axis=0)
        halves = [jnp.where(item == half, mask, 0.0) for half in range(2)]
        none = [jnp.zeros_like(mask)] * 2
        mask_ref[pair] = jnp.concatenate(
            [jnp.concatenate(halves + none, 1), jnp.concatenate(none + halves, 1)], 0
        ).astype(BF16)

    shape = upto_class.shape[1:]
    item = iota(shape, 1) // SUB
    part, half = item % LOW // 2, item % 2
    target = jnp.where(half == 0, part, jnp.where(part == 0, LOW // 2, LOW - part))
    sign = jnp.where((half == 1) & (part > 0), -1.0, 1.0)
    count = (half == 0) & (part == 0)

    def weight(m):
        beyond = jnp.where(count & (m > LOW // 2) & (m < LOW), 1.0, 0.0)
        return jnp.where(m == target, sign, 0.0) + beyond

    for b in range(BASINS):
        low = b * CLASSES - (first_high(b) + item // LOW) * LOW
        start, stop = jnp.maximum(low, 0), jnp.minimum(low + iota(shape, 0), LOW - 1) + 1
        upto_class[b] = jnp.where(stop > start, weight(start) - weight(stop), 0.0).astype(BF16)
    shape = upto_level.shape
    upto_level[...] = jnp.where(iota(shape, 0) <= iota(shape, 1), 1.0, 0.0).astype(BF16)
    shape = upto_row.shape
    a, b = iota(shape, 0), iota(shape, 1)
    upto_row[...] = jnp.where((a // rows == b // rows) & (b <= a), 1.0, 0.0).astype(BF16)


def gather_rows(blocks):
    row = iota(blocks[0].shape, 0)
    step = SUB // 2
    while step:
        low = row & step == 0
        joined = []
        for i in range(step):
            x, y = blocks[i], blocks[i + step]
            if step == SUB // 2:
                other = pltpu.roll(jnp.where(low, y, x), step, 0)
            else:
                other = jnp.where(low, pltpu.roll(x, SUB - step, 0), pltpu.roll(y, step, 0))
            joined.append(jnp.where(low, x, y) + other)
        blocks = joined
        step //= 2
    return blocks[0]


def pair_tables(sz, pair, north, up, dens, thick, coef, base_ref, mask_ref, flux, tab):
    highs, levels = sz["highs"], sz["levels"]
    zero = jnp.zeros((2 * SUB, 128), BF16)
    width = LOW * SUB
    own = iota((SUB, 128), 0) == iota((SUB, 128), 1) % SUB
    cells = pl.ds(pl.multiple_of(pair * 2 * SUB, 2 * SUB), 2 * SUB)

    lhs, rhs = ([], []), ([], [])
    kept = None
    for k in range(levels):
        depth_k = thick[k, cells, :].astype(F32)
        nf = north[k, cells, :].astype(F32) * (coef[0, cells, :] * depth_k)
        rf = up[k, cells, :].astype(F32) * (coef[1, cells, :] * jnp.minimum(depth_k, 1.0))
        if k % 2 == 1 or k == levels - 1:
            first = kept if k % 2 == 1 else (nf, rf)
            second = (nf, rf) if k % 2 == 1 else (jnp.zeros_like(nf),) * 2
            for s in range(2):
                for half in range(2):
                    part = slice(half * SUB, (half + 1) * SUB)
                    flux[2 * s + half, pl.ds(k // 2 * 2 * SUB, 2 * SUB), :] = jnp.concatenate(
                        [first[s][part], second[s][part]], 0
                    ).astype(BF16)
        kept = (nf, rf)
        q = base_ref[cells, :] + dens[k, cells, :]
        qf, lo = q.astype(F32), (q & (LOW - 1)).astype(F32)
        for half in range(2):
            part = slice(half * SUB, (half + 1) * SUB)
            join = lambda x, y: jnp.concatenate([x[part], y[part]], 0).astype(BF16)
            at_least = join(qf, qf - LOW)
            ends = join(lo, (LOW - 1) - lo)
            top = jnp.where(join(jnp.full_like(lo, LOW), lo) >= BF16(LOW // 2), BF16(1), zero)
            parts = [top] + [jnp.minimum(ends, BF16(p)) for p in range(1, LOW // 2)]
            rhs[half].append(jnp.concatenate(parts, 0).astype(F8))
            hits = [at_least >= BF16(2 * LOW * p) for p in range(highs // 2)]
            nd, rd = join(nf, nf), join(rf, rf)
            lhs[half].append(
                jnp.concatenate(
                    [jnp.where(h, nd, zero) for h in hits]
                    + [jnp.where(h, rd, zero) for h in hits],
                    0,
                )
            )
    sums = [
        lax.dot_general(
            jnp.concatenate(lhs[half], 1),
            jnp.concatenate(rhs[half], 1),
            NT,
            preferred_element_type=F32,
        )
        for half in range(2)
    ]
    seen = lax.dot_general(
        jnp.concatenate([flux[i] for i in range(4)], 1),
        mask_ref[pair],
        NT,
        preferred_element_type=F32,
    )

    def put(row, blocks):
        tab[row : row + SUB, :] = gather_rows([jnp.where(own, x, 0.0) for x in blocks])

    for half in range(2):
        for s in range(2):
            for c in range(width // 128):
                put(
                    class_row(half, s, c),
                    [
                        sums[half][(s * highs + h) * SUB :, c * 128 : (c + 1) * 128][:SUB]
                        for h in range(highs)
                    ],
                )
    for k in range(0, sz["even"], SUB):
        put(class_row(2, 0, 0) + k, [seen[(k + i) * SUB : (k + i + 1) * SUB] for i in range(SUB)])


def class_row(half, s, c):
    return ((half * 2 + s) * (LOW * SUB // 128) + c) * SUB


def table_rows(sz):
    return class_row(2, 0, 0) + sz["even"]


def kind_rows(sz, s, deep):
    at = (2 * s + deep) * sz["lanes"]
    return slice(at, at + sz["lanes"])


def month_sums(sz, total, consts, steps, mine):
    _, _, upto_class, upto_level, upto_row = consts
    rows, pairs, highs, span = sz["rows"], sz["pairs"], sz["highs"], sz["span"]
    width, wide = LOW * SUB, sz["wide"]
    row, lane = iota((SUB, 128), 0), iota((SUB, 128), 1)
    own = row == lane % SUB
    for pair in range(pairs):
        for s in range(2):
            exact = []
            for half in range(2):
                here, back = [], []
                for c in range(width // 128):
                    at = class_row(half, s, c)
                    x = total[pair][at : at + SUB]
                    x = x - jnp.where(row < highs - 1, pltpu.roll(x, SUB - 1, 0), 0.0)
                    here.append(x)
                    back.append(pltpu.roll(x, 2 * SUB, 1))
                for c in range(width // 128):
                    if c == 0:
                        turned = jnp.where(lane < 4 * SUB, 0.0, back[0])
                    else:
                        turned = jnp.where(lane < 2 * SUB, back[c - 1], back[c])
                    x = here[c] - turned
                    high = x.astype(BF16).astype(F32)
                    exact.append((high, x - high))
            for i in range(2):
                for h in range(highs):
                    for c in range(width // 128):
                        both = [exact[half * (width // 128) + c][i] for half in range(2)]
                        both = [
                            jnp.where(own, jnp.broadcast_to(x[h : h + 1], (SUB, 128)), 0.0)
                            for x in both
                        ]
                        at = (i * 2 + s) * rows + pair * 2 * SUB
                        steps[at : at + 2 * SUB, h * width + c * 128 : h * width + (c + 1) * 128] = (
                            jnp.concatenate(both, 0).astype(BF16)
                        )
    found = []
    for b in range(BASINS):
        cols = slice(first_high(b) * width, (first_high(b) + span) * width)
        x = lax.dot_general(steps[:, cols], upto_class[b], NT, preferred_element_type=F32)
        found.append(x[: 2 * rows] + x[2 * rows :])
    found = [sum(found[1:], found[0])] + found
    deep = []
    for pair in range(pairs):
        x = total[pair][class_row(2, 0, 0) :]
        deep.append(jnp.concatenate([x, jnp.zeros((wide - x.shape[0], 128), F32)], 0).T)
    for s in range(2):
        classes = jnp.concatenate([x[s * rows : (s + 1) * rows] for x in found], 0)
        levels = []
        for r in range(REGIONS):
            for pair in range(pairs):
                at = (s * REGIONS + r) * 2 * SUB
                levels.append(deep[pair][at : at + 2 * SUB])
        levels = jnp.concatenate(levels, 0)
        if s == 0:
            mine[kind_rows(sz, 0, 0), :] = classes
            mine[kind_rows(sz, 0, 1), :] = exact_dot(upto_level[...], levels, NN, False)
        else:
            mine[kind_rows(sz, 1, 0), :] = exact_dot(upto_row[...], classes, NN)
            mine[kind_rows(sz, 1, 1), :] = exact_dot(upto_row[...], levels, NN)


def const_shapes(sz, lons):
    lanes, wide = sz["lanes"], sz["wide"]
    return [
        pltpu.VMEM((sz["rows"], lons), jnp.int32),
        pltpu.VMEM((sz["pairs"], 2 * REGIONS * 2 * SUB, 4 * lons), BF16),
        pltpu.VMEM((BASINS, wide, sz["span"] * LOW * SUB), BF16),
        pltpu.VMEM((wide, wide), BF16),
        pltpu.VMEM((lanes, lanes), BF16),
    ]


def work_shapes(sz, lons):
    return [
        pltpu.VMEM((4, sz["even"] * SUB, lons), BF16),
        pltpu.VMEM((4 * sz["rows"], sz["highs"] * LOW * SUB), BF16),
    ]


def fused(sz, north_vel, up_vel, dens_class, thickness, basin_id):
    _, months, levels, rows, lons = north_vel.shape
    lanes, wide, pairs = sz["lanes"], sz["wide"], sz["pairs"]
    tall = 4 * lanes
    devices, lats, members = (lax.axis_size(a) for a in ("lon", "lat", "mem"))
    assert months == devices and sz["highs"] == SUB and lons == 128
    far = [(de, dl) for dl in range(1, lats) for de in range(members)]

    def kernel(north_h, up_h, dens_h, thick_h, basin_h, final, *scratch):
        consts, (flux, steps), rest = scratch[:5], scratch[5:7], scratch[7:]
        (north, up, dens, thick, basin, coef, tab, inbox, mine, membox, tail, tailbox, south) = rest[:13]
        in_sem, fix_sem, send, recv, msend, mrecv, tsend, trecv = rest[13:]
        me, lat, mem = (lax.axis_index(a) for a in ("lon", "lat", "mem"))

        def cells(pair):
            return pl.ds(pl.multiple_of(pair * 2 * SUB, 2 * SUB), 2 * SUB)

        def inputs(t, pair):
            month = lax.rem(me + 1 + t, devices)
            return [
                pltpu.make_async_copy(
                    h.at[0, month, :, cells(pair), :],
                    v.at[t, :, cells(pair), :],
                    in_sem.at[t, pair, i],
                )
                for i, (h, v) in enumerate(((north_h, north), (up_h, up), (dens_h, dens)))
            ]

        def layers(pair):
            return pltpu.make_async_copy(
                thick_h.at[:, cells(pair), :], thick.at[:, cells(pair), :], fix_sem.at[1 + pair]
            )

        fixed = pltpu.make_async_copy(basin_h, basin, fix_sem.at[0])
        fixed.start()
        for t in range(devices):
            for pair in range(pairs):
                for copy in ([layers(pair)] if t == 0 else []) + inputs(t, pair):
                    copy.start()

        barrier = pltpu.get_barrier_semaphore()
        peers = [{"lon": lax.rem(me + d, devices)} for d in range(1, devices)]
        peers += [
            {"lat": lax.rem(lat + dl, lats), "mem": lax.rem(mem + de, members)}
            for dl in range(lats)
            for de in range(members)
            if dl or de
        ]
        for peer in peers:
            pl.semaphore_signal(
                barrier, inc=1, device_id=peer, device_id_type=pl.DeviceIdType.MESH
            )

        index = lat * rows + iota((rows, lons), 0)
        latitude = (-78.0 + 156.0 * (index.astype(F32) + 0.5) / (rows * lats)) * (math.pi / 180.0)
        zonal = jnp.cos(latitude)
        coef[0] = (north_unit * 0.001) * zonal
        coef[1] = up_unit * zonal
        flux[:, levels * SUB :, :] = jnp.zeros_like(flux[:, levels * SUB :, :])
        south[...] = jnp.zeros_like(south)
        fixed.wait()
        prepare(sz, basin[...], consts)

        def table_copy(t, pair):
            return pltpu.make_async_remote_copy(
                src_ref=tab.at[t, pair],
                dst_ref=inbox.at[t, pair],
                send_sem=send.at[t, pair],
                recv_sem=recv.at[t, pair],
                device_id={"lon": lax.rem(me + 1 + t, devices)},
                device_id_type=pl.DeviceIdType.MESH,
            )

        def one_pair(i, carry):
            t, pair = i // pairs, lax.rem(i, pairs)

            @pl.when(t == 0)
            def _():
                layers(pair).wait()

            for copy in inputs(t, pair):
                copy.wait()
            pair_tables(
                sz,
                pair,
                north.at[t],
                up.at[t],
                dens.at[t],
                thick,
                coef,
                consts[0],
                consts[1],
                flux,
                tab.at[t, pair],
            )

            @pl.when(i == 0)
            def _():
                pl.semaphore_wait(barrier, len(peers))

            @pl.when(t < devices - 1)
            def _():
                table_copy(t, pair).start()

            return carry

        lax.fori_loop(0, devices * pairs, one_pair, 0)

        totals = []
        for pair in range(pairs):
            total = tab[devices - 1, pair]
            for t in range(devices - 1):
                table_copy(t, pair).wait_recv()
                total = total + inbox[t, pair]
            totals.append(total)
        month_sums(sz, totals, consts, steps, mine)
        copies = [
            pltpu.make_async_remote_copy(
                src_ref=mine,
                dst_ref=membox.at[de - 1],
                send_sem=msend.at[de - 1],
                recv_sem=mrecv.at[de - 1],
                device_id={"mem": lax.rem(mem + de, members)},
                device_id_type=pl.DeviceIdType.MESH,
            )
            for de in range(1, members)
        ]
        for copy in copies:
            copy.start()
        for deep in range(2):
            for r in range(REGIONS):
                at = kind_rows(sz, 1, deep).start + (r + 1) * rows - 1
                tail[deep * REGIONS + r : deep * REGIONS + r + 1, :] = mine[at : at + 1, :]

        def tail_copy(i, de, dl):
            return pltpu.make_async_remote_copy(
                src_ref=tail,
                dst_ref=tailbox.at[i],
                send_sem=tsend.at[i],
                recv_sem=trecv.at[i],
                device_id={"lat": lax.rem(lat + dl, lats), "mem": lax.rem(mem + de, members)},
                device_id_type=pl.DeviceIdType.MESH,
            )

        for i, (de, dl) in enumerate(far):

            @pl.when(lat + dl < lats)
            def _():
                tail_copy(i, de, dl).start()

        for i, (de, dl) in enumerate(far):

            @pl.when(lat >= dl)
            def _():
                tail_copy(i, de, dl).wait_recv()
                south[de] = south[de] + tailbox[i]

        for copy in copies:
            copy.wait_recv()
        for s in range(2):
            for deep in range(2):
                for r in range(REGIONS):
                    at = kind_rows(sz, s, deep).start + r * rows
                    part = []
                    for de in range(members):
                        whole = mine if de == 0 else membox.at[de - 1]
                        x = whole[at : at + rows, :]
                        if s == 1:
                            x = x + south[de, deep * REGIONS + r : deep * REGIONS + r + 1, :]
                        part.append(x)
                    mean = sum(part[1:], part[0]) / members
                    square = [jnp.square(x - mean) for x in part]
                    final[0, at : at + rows, :] = mean
                    final[1, at : at + rows, :] = jnp.sqrt(
                        sum(square[1:], square[0]) / (members - 1)
                    )

        for t in range(devices - 1):
            for pair in range(pairs):
                table_copy(t, pair).wait_send()
        for copy in copies:
            copy.wait_send()
        for i, (de, dl) in enumerate(far):

            @pl.when(lat + dl < lats)
            def _():
                tail_copy(i, de, dl).wait_send()

    slots = max(1, devices - 1)
    dma = pltpu.SemaphoreType.DMA
    table = (table_rows(sz), 128)
    tails = (2 * REGIONS, wide)
    return pl.pallas_call(
        kernel,
        out_shape=jax.ShapeDtypeStruct((2, tall, wide), F32),
        in_specs=[pl.BlockSpec(memory_space=pl.ANY)] * 5,
        out_specs=pl.BlockSpec(memory_space=pltpu.VMEM),
        scratch_shapes=const_shapes(sz, lons)
        + work_shapes(sz, lons)
        + [
            pltpu.VMEM((months, levels, rows, lons), north_vel.dtype),
            pltpu.VMEM((months, levels, rows, lons), up_vel.dtype),
            pltpu.VMEM((months, levels, rows, lons), dens_class.dtype),
            pltpu.VMEM((levels, rows, lons), thickness.dtype),
            pltpu.VMEM((rows, lons), basin_id.dtype),
            pltpu.VMEM((2, rows, lons), F32),
            pltpu.VMEM((devices, pairs) + table, F32),
            pltpu.VMEM((slots, pairs) + table, F32),
            pltpu.VMEM((tall, wide), F32),
            pltpu.VMEM((members - 1, tall, wide), F32),
            pltpu.VMEM(tails, F32),
            pltpu.VMEM((len(far),) + tails, F32),
            pltpu.VMEM((members,) + tails, F32),
            dma((devices, pairs, 3)),
            dma((1 + pairs,)),
            dma((slots, pairs)),
            dma((slots, pairs)),
            dma((members - 1,)),
            dma((members - 1,)),
            dma((len(far),)),
            dma((len(far),)),
        ],
        compiler_params=pltpu.CompilerParams(
            collective_id=0, has_side_effects=True, vmem_limit_bytes=60 * 2**20
        ),
    )(north_vel, up_vel, dens_class, thickness, basin_id)


def place(sz, final):
    rows, levels = sz["rows"], sz["levels"]

    def kernel(final, *outs):
        for s in range(2):
            for deep, count in ((1, levels), (0, CLASSES)):
                for i in range(2):
                    for r in range(REGIONS):
                        at = kind_rows(sz, s, deep).start + r * rows
                        o = outs[i + 2 * (1 - deep)]
                        o[0, r, s] = final[i, at : at + rows, :count]

    out = lambda n: jax.ShapeDtypeStruct((1, REGIONS, 2, rows, n), F32)
    outs = pl.pallas_call(
        kernel,
        out_shape=[out(levels), out(levels), out(CLASSES), out(CLASSES)],
        in_specs=[pl.BlockSpec(memory_space=pltpu.VMEM)],
        out_specs=[pl.BlockSpec(memory_space=pltpu.VMEM)] * 4,
    )(final)
    return tuple(jnp.swapaxes(x, 3, 4) for x in outs)


def body(north_vel, up_vel, dens_class, thickness, basin_id):
    levels, rows = north_vel.shape[2:4]
    sz = sizes_of(levels, rows)
    return place(sz, fused(sz, north_vel, up_vel, dens_class, thickness, basin_id))


def solution(mesh):
    in_specs = (
        P("mem", None, None, "lat", "lon"),
        P("mem", None, None, "lat", "lon"),
        P("mem", None, None, "lat", "lon"),
        P(None, "lat", "lon"),
        P("lat", "lon"),
    )
    out_specs = (P("lon", None, None, None, "lat"),) * 4
    return jax.shard_map(body, mesh=mesh, in_specs=in_specs, out_specs=out_specs, check_vma=False)
```

time: 32.8 us -> 25.5 us (0.78)
  Pallas kernels: 32 us -> 24.7 us
    pallas_call x2, Pallas kernels: 32 us -> 24.7 us  [the longest x1 22.9 us: fused(): pl.pallas_call(kernel, out_shape=jax.ShapeDtypeStruct((2, tall, wide), F3...]
where the time goes in v1:
time: 25.5 us; the launch traced here: 25.4 us
  Pallas kernels  24.7 us (97%)
  between operations  0.64 us (3%)
    pallas_call x1, Pallas kernels, fused(): pl.pallas_call(kernel, out_shape=jax.ShapeDtypeStruct((2, tall, wide), F3...  22.9 us
    pallas_call x1, Pallas kernels, place(): pl.pallas_call(kernel, out_shape=[out(levels), out(levels), out(CLASSES),...  1.84 us

profile of v1, /device:TPU:0, one launch (start us, length us, event | category | flops | bytes accessed | tf_op | source)
XLA Modules:
  0.0 25.4 jit_solution(17941705874618665247)
XLA Ops:
  0.6 22.9 %shard_map.84.final = f32[2,512,128]{2,1,0:T(8,128)} custom-call(bf16[1,4,75,32,128]{4,3,2,1,0:T(8,128)(2,1)} %north_h.1, bf16[1,4,75,32,128]{4,3,2,1,0:T(8,128)(2,1)} %up_h.1, s32[1,4,75,32,128]{4,3,2,1,0:T(8,128)} %dens_h.1, s32[75,32,128]{2,1,0:T(8,128)} %thick_h.1, s32[32,128]{1,0:T(8,128)} %basin_h.1), custom_call_target="tpu_custom_call" | custom-call | tf_op jit(solution)/shard_map/pallas_call | solution.py:483
  23.5 1.8 %shard_map.85 = (f32[1,4,2,32,75]{4,3,2,1,0:T(8,128)}, f32[1,4,2,32,75]{4,3,2,1,0:T(8,128)}, f32[1,4,2,32,80]{4,3,2,1,0:T(8,128)}, f32[1,4,2,32,80]{4,3,2,1,0:T(8,128)}) custom-call(f32[2,512,128]{2,1,0:T(8,128)} %shard_map.84.final), custom_call_target="tpu_custom_call" | custom-call | tf_op jit(solution)/shard_map/pallas_call | solution.py:532

commit v2 on v1

--- a/solution.py
+++ b/solution.py
@@ -80,7 +80,7 @@
         ).astype(BF16)
 
     shape = upto_class.shape[1:]
-    item = iota(shape, 1) // SUB
+    item = iota(shape, 0) // SUB
     part, half = item % LOW // 2, item % 2
     target = jnp.where(half == 0, part, jnp.where(part == 0, LOW // 2, LOW - part))
     sign = jnp.where((half == 1) & (part > 0), -1.0, 1.0)
@@ -92,7 +92,7 @@
 
     for b in range(BASINS):
         low = b * CLASSES - (first_high(b) + item // LOW) * LOW
-        start, stop = jnp.maximum(low, 0), jnp.minimum(low + iota(shape, 0), LOW - 1) + 1
+        start, stop = jnp.maximum(low, 0), jnp.minimum(low + iota(shape, 1), LOW - 1) + 1
         upto_class[b] = jnp.where(stop > start, weight(start) - weight(stop), 0.0).astype(BF16)
     shape = upto_level.shape
     upto_level[...] = jnp.where(iota(shape, 0) <= iota(shape, 1), 1.0, 0.0).astype(BF16)
@@ -207,7 +207,7 @@
     return slice(at, at + sz["lanes"])
 
 
-def month_sums(sz, total, consts, steps, mine):
+def month_sums(sz, total, consts, steps, mine, send_part):
     _, _, upto_class, upto_level, upto_row = consts
     rows, pairs, highs, span = sz["rows"], sz["pairs"], sz["highs"], sz["span"]
     width, wide = LOW * SUB, sz["wide"]
@@ -247,7 +247,7 @@
     found = []
     for b in range(BASINS):
         cols = slice(first_high(b) * width, (first_high(b) + span) * width)
-        x = lax.dot_general(steps[:, cols], upto_class[b], NT, preferred_element_type=F32)
+        x = lax.dot_general(steps[:, cols], upto_class[b], NN, preferred_element_type=F32)
         found.append(x[: 2 * rows] + x[2 * rows :])
     found = [sum(found[1:], found[0])] + found
     deep = []
@@ -262,12 +262,15 @@
                 at = (s * REGIONS + r) * 2 * SUB
                 levels.append(deep[pair][at : at + 2 * SUB])
         levels = jnp.concatenate(levels, 0)
+        lanes = sz["lanes"]
         if s == 0:
-            mine[kind_rows(sz, 0, 0), :] = classes
-            mine[kind_rows(sz, 0, 1), :] = exact_dot(upto_level[...], levels, NN, False)
+            levels = exact_dot(upto_level[...], levels, NN, False)
         else:
-            mine[kind_rows(sz, 1, 0), :] = exact_dot(upto_row[...], classes, NN)
-            mine[kind_rows(sz, 1, 1), :] = exact_dot(upto_row[...], levels, NN)
+            classes = exact_dot(upto_row[...], classes, NN)
+            levels = exact_dot(upto_row[...], levels, NN)
+        mine[s, :lanes, :] = classes
+        mine[s, lanes:, :] = levels
+        send_part(s)
 
 
 def const_shapes(sz, lons):
@@ -275,7 +278,7 @@
     return [
         pltpu.VMEM((sz["rows"], lons), jnp.int32),
         pltpu.VMEM((sz["pairs"], 2 * REGIONS * 2 * SUB, 4 * lons), BF16),
-        pltpu.VMEM((BASINS, wide, sz["span"] * LOW * SUB), BF16),
+        pltpu.VMEM((BASINS, sz["span"] * LOW * SUB, wide), BF16),
         pltpu.VMEM((wide, wide), BF16),
         pltpu.VMEM((lanes, lanes), BF16),
     ]
@@ -305,8 +308,20 @@
         def cells(pair):
             return pl.ds(pl.multiple_of(pair * 2 * SUB, 2 * SUB), 2 * SUB)
 
+        orders = [
+            sorted((d for d in range(devices) if d != e), key=lambda d: (d != devices - 1 - e, d))
+            for e in range(devices)
+        ]
+
+        def month_at(t):
+            month = me
+            for e, order in enumerate(orders):
+                for turn, d in enumerate(order):
+                    month = jnp.where((me == e) & (t == turn), d, month)
+            return month
+
         def inputs(t, pair):
-            month = lax.rem(me + 1 + t, devices)
+            month = month_at(t)
             return [
                 pltpu.make_async_copy(
                     h.at[0, month, :, cells(pair), :],
@@ -323,10 +338,10 @@
 
         fixed = pltpu.make_async_copy(basin_h, basin, fix_sem.at[0])
         fixed.start()
-        for t in range(devices):
-            for pair in range(pairs):
-                for copy in ([layers(pair)] if t == 0 else []) + inputs(t, pair):
-                    copy.start()
+        steps_ahead = min(2, devices * pairs)
+        layers(0).start()
+        for copy in inputs(0, 0):
+            copy.start()
 
         barrier = pltpu.get_barrier_semaphore()
         peers = [{"lon": lax.rem(me + d, devices)} for d in range(1, devices)]
@@ -350,19 +365,48 @@
         south[...] = jnp.zeros_like(south)
         fixed.wait()
         prepare(sz, basin[...], consts)
+        for i in range(1, steps_ahead):
+            for copy in ([layers(i)] if i < pairs else []) + inputs(i // pairs, i % pairs):
+                copy.start()
 
         def table_copy(t, pair):
+            owner = month_at(t)
+            slot = lax.rem(owner - me + devices, devices) - 1
             return pltpu.make_async_remote_copy(
                 src_ref=tab.at[t, pair],
-                dst_ref=inbox.at[t, pair],
+                dst_ref=inbox.at[slot, pair],
                 send_sem=send.at[t, pair],
-                recv_sem=recv.at[t, pair],
-                device_id={"lon": lax.rem(me + 1 + t, devices)},
+                recv_sem=recv.at[slot, pair],
+                device_id={"lon": owner},
                 device_id_type=pl.DeviceIdType.MESH,
             )
 
+        def arrival(slot, pair):
+            return pltpu.make_async_remote_copy(
+                src_ref=tab.at[0, pair],
+                dst_ref=inbox.at[slot, pair],
+                send_sem=send.at[0, pair],
+                recv_sem=recv.at[slot, pair],
+                device_id={"lon": lax.rem(me + 1, devices)},
+                device_id_type=pl.DeviceIdType.MESH,
+            )
+
+        hold = min(2, (devices - 1) * pairs - 1)
+
         def one_pair(i, carry):
             t, pair = i // pairs, lax.rem(i, pairs)
+
+            @pl.when(i + steps_ahead < devices * pairs)
+            def _():
+                later = i + steps_ahead
+                for copy in inputs(later // pairs, lax.rem(later, pairs)):
+                    copy.start()
+
+            if steps_ahead < pairs:
+
+                @pl.when(i + steps_ahead < pairs)
+                def _():
+                    layers(i + steps_ahead).start()
 
             @pl.when(t == 0)
             def _():
@@ -384,11 +428,13 @@
                 tab.at[t, pair],
             )
 
-            @pl.when(i == 0)
+            @pl.when(i == hold)
             def _():
                 pl.semaphore_wait(barrier, len(peers))
-
-            @pl.when(t < devices - 1)
+                for j in range(hold):
+                    table_copy(j // pairs, j % pairs).start()
+
+            @pl.when((i >= hold) & (t < devices - 1))
             def _():
                 table_copy(t, pair).start()
 
@@ -400,27 +446,33 @@
         for pair in range(pairs):
             total = tab[devices - 1, pair]
             for t in range(devices - 1):
-                table_copy(t, pair).wait_recv()
+                arrival(t, pair).wait_recv()
                 total = total + inbox[t, pair]
             totals.append(total)
-        month_sums(sz, totals, consts, steps, mine)
         copies = [
-            pltpu.make_async_remote_copy(
-                src_ref=mine,
-                dst_ref=membox.at[de - 1],
-                send_sem=msend.at[de - 1],
-                recv_sem=mrecv.at[de - 1],
-                device_id={"mem": lax.rem(mem + de, members)},
-                device_id_type=pl.DeviceIdType.MESH,
-            )
-            for de in range(1, members)
+            [
+                pltpu.make_async_remote_copy(
+                    src_ref=mine.at[s],
+                    dst_ref=membox.at[de - 1, s],
+                    send_sem=msend.at[de - 1, s],
+                    recv_sem=mrecv.at[de - 1, s],
+                    device_id={"mem": lax.rem(mem + de, members)},
+                    device_id_type=pl.DeviceIdType.MESH,
+                )
+                for de in range(1, members)
+            ]
+            for s in range(2)
         ]
-        for copy in copies:
-            copy.start()
+
+        def send_part(s):
+            for copy in copies[s]:
+                copy.start()
+
+        month_sums(sz, totals, consts, steps, mine, send_part)
         for deep in range(2):
             for r in range(REGIONS):
-                at = kind_rows(sz, 1, deep).start + (r + 1) * rows - 1
-                tail[deep * REGIONS + r : deep * REGIONS + r + 1, :] = mine[at : at + 1, :]
+                at = deep * lanes + (r + 1) * rows - 1
+                tail[deep * REGIONS + r : deep * REGIONS + r + 1, :] = mine[1, at : at + 1, :]
 
         def tail_copy(i, de, dl):
             return pltpu.make_async_remote_copy(
@@ -438,28 +490,30 @@
             def _():
                 tail_copy(i, de, dl).start()
 
-        for i, (de, dl) in enumerate(far):
-
-            @pl.when(lat >= dl)
-            def _():
-                tail_copy(i, de, dl).wait_recv()
-                south[de] = south[de] + tailbox[i]
-
-        for copy in copies:
-            copy.wait_recv()
         for s in range(2):
+            if s == 1:
+                for i, (de, dl) in enumerate(far):
+
+                    @pl.when(lat >= dl)
+                    def _():
+                        tail_copy(i, de, dl).wait_recv()
+                        south[de] = south[de] + tailbox[i]
+
+            for copy in copies[s]:
+                copy.wait_recv()
             for deep in range(2):
                 for r in range(REGIONS):
-                    at = kind_rows(sz, s, deep).start + r * rows
+                    at = deep * lanes + r * rows
                     part = []
                     for de in range(members):
-                        whole = mine if de == 0 else membox.at[de - 1]
+                        whole = mine.at[s] if de == 0 else membox.at[de - 1, s]
                         x = whole[at : at + rows, :]
                         if s == 1:
                             x = x + south[de, deep * REGIONS + r : deep * REGIONS + r + 1, :]
                         part.append(x)
                     mean = sum(part[1:], part[0]) / members
                     square = [jnp.square(x - mean) for x in part]
+                    at += s * 2 * lanes
                     final[0, at : at + rows, :] = mean
                     final[1, at : at + rows, :] = jnp.sqrt(
                         sum(square[1:], square[0]) / (members - 1)
@@ -468,7 +522,7 @@
         for t in range(devices - 1):
             for pair in range(pairs):
                 table_copy(t, pair).wait_send()
-        for copy in copies:
+        for copy in copies[0] + copies[1]:
             copy.wait_send()
         for i, (de, dl) in enumerate(far):
 
@@ -476,6 +530,7 @@
             def _():
                 tail_copy(i, de, dl).wait_send()
 
+    arrays = (north_vel, up_vel, dens_class, thickness, basin_id)
     slots = max(1, devices - 1)
     dma = pltpu.SemaphoreType.DMA
     table = (table_rows(sz), 128)
@@ -496,8 +551,8 @@
             pltpu.VMEM((2, rows, lons), F32),
             pltpu.VMEM((devices, pairs) + table, F32),
             pltpu.VMEM((slots, pairs) + table, F32),
-            pltpu.VMEM((tall, wide), F32),
-            pltpu.VMEM((members - 1, tall, wide), F32),
+            pltpu.VMEM((2, 2 * lanes, wide), F32),
+            pltpu.VMEM((members - 1, 2, 2 * lanes, wide), F32),
             pltpu.VMEM(tails, F32),
             pltpu.VMEM((len(far),) + tails, F32),
             pltpu.VMEM((members,) + tails, F32),
@@ -505,15 +560,15 @@
             dma((1 + pairs,)),
             dma((slots, pairs)),
             dma((slots, pairs)),
-            dma((members - 1,)),
-            dma((members - 1,)),
+            dma((members - 1, 2)),
+            dma((members - 1, 2)),
             dma((len(far),)),
             dma((len(far),)),
         ],
         compiler_params=pltpu.CompilerParams(
-            collective_id=0, has_side_effects=True, vmem_limit_bytes=60 * 2**20
+            collective_id=0, has_side_effects=True, vmem_limit_bytes=44 * 2**20
         ),
-    )(north_vel, up_vel, dens_class, thickness, basin_id)
+    )(*[pltpu.with_memory_space_constraint(x, pltpu.HBM) for x in arrays])
 
 
 def place(sz, final):
@@ -534,6 +589,7 @@
         out_shape=[out(levels), out(levels), out(CLASSES), out(CLASSES)],
         in_specs=[pl.BlockSpec(memory_space=pltpu.VMEM)],
         out_specs=[pl.BlockSpec(memory_space=pltpu.VMEM)] * 4,
+        compiler_params=pltpu.CompilerParams(vmem_limit_bytes=8 * 2**20),
     )(final)
     return tuple(jnp.swapaxes(x, 3, 4) for x in outs)
 

time: 25.5 us -> 21.3 us (0.84)
  Pallas kernels: 24.7 us -> 20.4 us
    pallas_call x1, Pallas kernels: 22.9 us -> 19.6 us  [fused(): pl.pallas_call(kernel, out_shape=jax.ShapeDtypeStruct((2, tall, wide), F3...]
    pallas_call x1, Pallas kernels: 1.84 us -> 0.82 us  [place(): pl.pallas_call(kernel, out_shape=[out(levels), out(levels), out(CLASSES),...]
where the time goes in v2:
time: 21.3 us; the launch traced here: 21 us
  Pallas kernels  20.4 us (96%)
  between operations  0.64 us (3%)
    pallas_call x1, Pallas kernels, fused(): pl.pallas_call(kernel, out_shape=jax.ShapeDtypeStruct((2, tall, wide), F3...  19.6 us
    pallas_call x1, Pallas kernels, place(): pl.pallas_call(kernel, out_shape=[out(levels), out(levels), out(CLASSES),...  0.82 us

profile of v2, /device:TPU:0, one launch (start us, length us, event | category | flops | bytes accessed | tf_op | source)
XLA Modules:
  0.0 21.0 jit_solution(16233386383326200819)
XLA Ops:
  0.6 19.6 %shard_map.84.final = f32[2,512,128]{2,1,0:T(8,128)S(1)} custom-call(bf16[1,4,75,32,128]{4,3,2,1,0:T(8,128)(2,1)} %north_h.1, bf16[1,4,75,32,128]{4,3,2,1,0:T(8,128)(2,1)} %up_h.1, s32[1,4,75,32,128]{4,3,2,1,0:T(8,128)} %dens_h.1, s32[75,32,128]{2,1,0:T(8,128)} %thick_h.1, s32[32,128]{1,0:T(8,128)} %basin_h.1), custom_call_target="tpu_custom_call" | custom-call | tf_op jit(solution)/shard_map/pallas_call | solution.py:538
  20.2 0.8 %shard_map.85 = (f32[1,4,2,32,75]{4,3,2,1,0:T(8,128)}, f32[1,4,2,32,75]{4,3,2,1,0:T(8,128)}, f32[1,4,2,32,80]{4,3,2,1,0:T(8,128)}, f32[1,4,2,32,80]{4,3,2,1,0:T(8,128)}) custom-call(f32[2,512,128]{2,1,0:T(8,128)S(1)} %shard_map.84.final), custom_call_target="tpu_custom_call" | custom-call | tf_op jit(solution)/shard_map/pallas_call | solution.py:587

commit v3 on v2

--- a/solution.py
+++ b/solution.py
@@ -53,7 +53,7 @@
         pairs=rows // (2 * SUB),
         highs=-(-BASINS * CLASSES // LOW),
         span=-(-CLASSES // LOW),
-        even=round_up(levels, SUB),
+        near=round_up(-(-levels // 2), 2),
         wide=round_up(max(levels, CLASSES), 128),
         lanes=REGIONS * rows,
     )
@@ -63,42 +63,59 @@
     return b * CLASSES // LOW
 
 
-def prepare(sz, basin, consts):
-    base_ref, mask_ref, upto_class, upto_level, upto_row = consts
+def prepare_weights(sz, consts):
+    _, _, upto_class, upto_level, upto_row = consts
     rows = sz["rows"]
-    base_ref[...] = jnp.where(basin > 0, (basin - 1) * CLASSES, -LOW * 64)
-    regions = [basin > 0] + [basin == r for r in range(1, REGIONS)]
-    regions = [jnp.where(r, 1.0, 0.0) for r in regions]
-    item = iota((REGIONS * 2 * SUB, basin.shape[1]), 0) % (2 * SUB) // SUB
-    for pair in range(sz["pairs"]):
-        cells = slice(pair * 2 * SUB, (pair + 1) * 2 * SUB)
-        mask = jnp.concatenate([r[cells] for r in regions], axis=0)
-        halves = [jnp.where(item == half, mask, 0.0) for half in range(2)]
-        none = [jnp.zeros_like(mask)] * 2
-        mask_ref[pair] = jnp.concatenate(
-            [jnp.concatenate(halves + none, 1), jnp.concatenate(none + halves, 1)], 0
-        ).astype(BF16)
-
-    shape = upto_class.shape[1:]
-    item = iota(shape, 0) // SUB
-    part, half = item % LOW // 2, item % 2
-    target = jnp.where(half == 0, part, jnp.where(part == 0, LOW // 2, LOW - part))
-    sign = jnp.where((half == 1) & (part > 0), -1.0, 1.0)
-    count = (half == 0) & (part == 0)
-
-    def weight(m):
-        beyond = jnp.where(count & (m > LOW // 2) & (m < LOW), 1.0, 0.0)
-        return jnp.where(m == target, sign, 0.0) + beyond
-
+    wide = upto_class.shape[2]
+    c = iota((SUB, wide), 1)
     for b in range(BASINS):
-        low = b * CLASSES - (first_high(b) + item // LOW) * LOW
-        start, stop = jnp.maximum(low, 0), jnp.minimum(low + iota(shape, 1), LOW - 1) + 1
-        upto_class[b] = jnp.where(stop > start, weight(start) - weight(stop), 0.0).astype(BF16)
+        for h in range(sz["span"]):
+            low = b * CLASSES - (first_high(b) + h) * LOW
+            start = max(low, 0)
+            stop = jnp.minimum(c + (low + 1), LOW)
+            some = stop > start
+            beyond = some & (stop > LOW // 2) & (stop < LOW)
+            for part in range(LOW // 2):
+                both = []
+                for half in range(2):
+                    target = part if half == 0 else (LOW - part if part else LOW // 2)
+                    sign = -1.0 if half == 1 and part else 1.0
+                    first = sign if start == target else 0.0
+                    x = jnp.where(some, first - jnp.where(stop == target, sign, 0.0), 0.0)
+                    if half == 0 and part == 0:
+                        if LOW // 2 < start < LOW:
+                            x = x + jnp.where(some, 1.0, 0.0)
+                        x = x - jnp.where(beyond, 1.0, 0.0)
+                    both.append(x)
+                at = (h * LOW + 2 * part) * SUB
+                upto_class[b, at : at + 2 * SUB, :] = jnp.concatenate(both, 0).astype(BF16)
     shape = upto_level.shape
     upto_level[...] = jnp.where(iota(shape, 0) <= iota(shape, 1), 1.0, 0.0).astype(BF16)
     shape = upto_row.shape
     a, b = iota(shape, 0), iota(shape, 1)
     upto_row[...] = jnp.where((a // rows == b // rows) & (b <= a), 1.0, 0.0).astype(BF16)
+
+
+def prepare_masks(sz, basin, consts):
+    base_ref, mask_ref = consts[:2]
+    lons = basin.shape[1]
+    base_ref[...] = jnp.where(basin > 0, (basin - 1) * CLASSES, -LOW * 64)
+    regions = [basin > 0] + [basin == r for r in range(1, REGIONS)]
+    regions = [jnp.where(r, 1.0, 0.0) for r in regions]
+    lane = iota((lons, 2 * REGIONS * 2 * SUB), 1)
+    none = jnp.zeros(lane.shape, BF16)
+    for pair in range(sz["pairs"]):
+        cells = slice(pair * 2 * SUB, (pair + 1) * 2 * SUB)
+        mask = jnp.concatenate([r[cells] for r in regions] * 2, axis=0).T
+        for s in range(2):
+            for half in range(2):
+                here = (lane // (REGIONS * 2 * SUB) == s) & (lane // SUB % 2 == half)
+                here = jnp.where(here, mask, 0.0).astype(BF16)
+                for late in range(2):
+                    at = (late * 4 + 2 * s + half) * lons
+                    mask_ref[pair, at : at + lons, :] = jnp.concatenate(
+                        [none, here] if late else [here, none], 1
+                    )
 
 
 def gather_rows(blocks):
@@ -170,10 +187,11 @@
         )
         for half in range(2)
     ]
+    near = sz["near"] * SUB
     seen = lax.dot_general(
-        jnp.concatenate([flux[i] for i in range(4)], 1),
+        jnp.concatenate([flux[i, late * near : (late + 1) * near, :] for late in range(2) for i in range(4)], 1),
         mask_ref[pair],
-        NT,
+        NN,
         preferred_element_type=F32,
     )
 
@@ -190,8 +208,15 @@
                         for h in range(highs)
                     ],
                 )
-    for k in range(0, sz["even"], SUB):
-        put(class_row(2, 0, 0) + k, [seen[(k + i) * SUB : (k + i + 1) * SUB] for i in range(SUB)])
+
+    def level(k):
+        if k >= levels:
+            return jnp.zeros((SUB, 128), F32)
+        late, k = divmod(k, sz["near"])
+        return seen[k * SUB : (k + 1) * SUB, late * 128 : (late + 1) * 128]
+
+    for k in range(0, levels, SUB):
+        put(class_row(2, 0, 0) + k, [level(k + i) for i in range(SUB)])
 
 
 def class_row(half, s, c):
@@ -199,7 +224,7 @@
 
 
 def table_rows(sz):
-    return class_row(2, 0, 0) + sz["even"]
+    return class_row(2, 0, 0) + round_up(sz["levels"], SUB)
 
 
 def kind_rows(sz, s, deep):
@@ -207,7 +232,7 @@
     return slice(at, at + sz["lanes"])
 
 
-def month_sums(sz, total, consts, steps, mine, send_part):
+def month_sums(sz, total, consts, steps, mine, send_tail, send_part):
     _, _, upto_class, upto_level, upto_row = consts
     rows, pairs, highs, span = sz["rows"], sz["pairs"], sz["highs"], sz["span"]
     width, wide = LOW * SUB, sz["wide"]
@@ -254,6 +279,7 @@
     for pair in range(pairs):
         x = total[pair][class_row(2, 0, 0) :]
         deep.append(jnp.concatenate([x, jnp.zeros((wide - x.shape[0], 128), F32)], 0).T)
+    tables = []
     for s in range(2):
         classes = jnp.concatenate([x[s * rows : (s + 1) * rows] for x in found], 0)
         levels = []
@@ -261,8 +287,17 @@
             for pair in range(pairs):
                 at = (s * REGIONS + r) * 2 * SUB
                 levels.append(deep[pair][at : at + 2 * SUB])
-        levels = jnp.concatenate(levels, 0)
-        lanes = sz["lanes"]
+        tables.append((classes, jnp.concatenate(levels, 0)))
+    send_tail(
+        [
+            jnp.sum(x[r * rows : (r + 1) * rows], axis=0, keepdims=True)
+            for x in tables[1]
+            for r in range(REGIONS)
+        ]
+    )
+    lanes = sz["lanes"]
+    for s in range(2):
+        classes, levels = tables[s]
         if s == 0:
             levels = exact_dot(upto_level[...], levels, NN, False)
         else:
@@ -277,7 +312,7 @@
     lanes, wide = sz["lanes"], sz["wide"]
     return [
         pltpu.VMEM((sz["rows"], lons), jnp.int32),
-        pltpu.VMEM((sz["pairs"], 2 * REGIONS * 2 * SUB, 4 * lons), BF16),
+        pltpu.VMEM((sz["pairs"], 8 * lons, 2 * 2 * REGIONS * 2 * SUB), BF16),
         pltpu.VMEM((BASINS, sz["span"] * LOW * SUB, wide), BF16),
         pltpu.VMEM((wide, wide), BF16),
         pltpu.VMEM((lanes, lanes), BF16),
@@ -286,7 +321,7 @@
 
 def work_shapes(sz, lons):
     return [
-        pltpu.VMEM((4, sz["even"] * SUB, lons), BF16),
+        pltpu.VMEM((4, 2 * sz["near"] * SUB, lons), BF16),
         pltpu.VMEM((4 * sz["rows"], sz["highs"] * LOW * SUB), BF16),
     ]
 
@@ -363,8 +398,9 @@
         coef[1] = up_unit * zonal
         flux[:, levels * SUB :, :] = jnp.zeros_like(flux[:, levels * SUB :, :])
         south[...] = jnp.zeros_like(south)
+        prepare_weights(sz, consts)
         fixed.wait()
-        prepare(sz, basin[...], consts)
+        prepare_masks(sz, basin[...], consts)
         for i in range(1, steps_ahead):
             for copy in ([layers(i)] if i < pairs else []) + inputs(i // pairs, i % pairs):
                 copy.start()
@@ -391,7 +427,7 @@
                 device_id_type=pl.DeviceIdType.MESH,
             )
 
-        hold = min(2, (devices - 1) * pairs - 1)
+        hold = min(1, (devices - 1) * pairs - 1)
 
         def one_pair(i, carry):
             t, pair = i // pairs, lax.rem(i, pairs)
@@ -468,12 +504,6 @@
             for copy in copies[s]:
                 copy.start()
 
-        month_sums(sz, totals, consts, steps, mine, send_part)
-        for deep in range(2):
-            for r in range(REGIONS):
-                at = deep * lanes + (r + 1) * rows - 1
-                tail[deep * REGIONS + r : deep * REGIONS + r + 1, :] = mine[1, at : at + 1, :]
-
         def tail_copy(i, de, dl):
             return pltpu.make_async_remote_copy(
                 src_ref=tail,
@@ -484,12 +514,16 @@
                 device_id_type=pl.DeviceIdType.MESH,
             )
 
-        for i, (de, dl) in enumerate(far):
-
-            @pl.when(lat + dl < lats)
-            def _():
-                tail_copy(i, de, dl).start()
-
+        def send_tail(lines):
+            for r, line in enumerate(lines):
+                tail[r : r + 1, :] = line
+            for i, (de, dl) in enumerate(far):
+
+                @pl.when(lat + dl < lats)
+                def _():
+                    tail_copy(i, de, dl).start()
+
+        month_sums(sz, totals, consts, steps, mine, send_tail, send_part)
         for s in range(2):
             if s == 1:
                 for i, (de, dl) in enumerate(far):

time: 21.3 us -> 20.7 us (0.972)
  the two profiles are of different devices: /device:TPU:0 before, /device:TPU:21 now
where the time goes in v3:
time: 20.7 us; the launch traced here: 20.5 us
  Pallas kernels  19.9 us (96%)
  between operations  0.64 us (3%)
    pallas_call x1, Pallas kernels, fused(): pl.pallas_call(kernel, out_shape=jax.ShapeDtypeStruct((2, tall, wide), F3...  19 us
    pallas_call x1, Pallas kernels, place(): pl.pallas_call(kernel, out_shape=[out(levels), out(levels), out(CLASSES),...  0.82 us

profile of v3, /device:TPU:21, one launch (start us, length us, event | category | flops | bytes accessed | tf_op | source)
XLA Modules:
  0.0 20.5 jit_solution(18022711499379776335)
XLA Ops:
  0.6 19.0 %shard_map.84.final = f32[2,512,128]{2,1,0:T(8,128)S(1)} custom-call(bf16[1,4,75,32,128]{4,3,2,1,0:T(8,128)(2,1)} %north_h.1, bf16[1,4,75,32,128]{4,3,2,1,0:T(8,128)(2,1)} %up_h.1, s32[1,4,75,32,128]{4,3,2,1,0:T(8,128)} %dens_h.1, s32[75,32,128]{2,1,0:T(8,128)} %thick_h.1, s32[32,128]{1,0:T(8,128)} %basin_h.1), custom_call_target="tpu_custom_call" | custom-call | tf_op jit(solution)/shard_map/pallas_call | solution.py:572
  19.7 0.8 %shard_map.85 = (f32[1,4,2,32,75]{4,3,2,1,0:T(8,128)}, f32[1,4,2,32,75]{4,3,2,1,0:T(8,128)}, f32[1,4,2,32,80]{4,3,2,1,0:T(8,128)}, f32[1,4,2,32,80]{4,3,2,1,0:T(8,128)}) custom-call(f32[2,512,128]{2,1,0:T(8,128)S(1)} %shard_map.84.final), custom_call_target="tpu_custom_call" | custom-call | tf_op jit(solution)/shard_map/pallas_call | solution.py:621

commit v4 on v3

--- a/solution.py
+++ b/solution.py
@@ -141,7 +141,8 @@
     zero = jnp.zeros((2 * SUB, 128), BF16)
     width = LOW * SUB
     own = iota((SUB, 128), 0) == iota((SUB, 128), 1) % SUB
-    cells = pl.ds(pl.multiple_of(pair * 2 * SUB, 2 * SUB), 2 * SUB)
+    start = pair * 2 * SUB
+    cells = pl.ds(start if isinstance(pair, int) else pl.multiple_of(start, 2 * SUB), 2 * SUB)
 
     lhs, rhs = ([], []), ([], [])
     kept = None
@@ -296,15 +297,13 @@
         ]
     )
     lanes = sz["lanes"]
+    done = [
+        (tables[0][0], exact_dot(upto_level[...], tables[0][1], NN, False)),
+        tuple(exact_dot(upto_row[...], x, NN) for x in tables[1]),
+    ]
     for s in range(2):
-        classes, levels = tables[s]
-        if s == 0:
-            levels = exact_dot(upto_level[...], levels, NN, False)
-        else:
-            classes = exact_dot(upto_row[...], classes, NN)
-            levels = exact_dot(upto_row[...], levels, NN)
-        mine[s, :lanes, :] = classes
-        mine[s, lanes:, :] = levels
+        mine[s, :lanes, :], mine[s, lanes:, :] = done[s]
+    for s in range(2):
         send_part(s)
 
 
@@ -321,7 +320,7 @@
 
 def work_shapes(sz, lons):
     return [
-        pltpu.VMEM((4, 2 * sz["near"] * SUB, lons), BF16),
+        pltpu.VMEM((sz["pairs"], 4, 2 * sz["near"] * SUB, lons), BF16),
         pltpu.VMEM((4 * sz["rows"], sz["highs"] * LOW * SUB), BF16),
     ]
 
@@ -332,7 +331,7 @@
     tall = 4 * lanes
     devices, lats, members = (lax.axis_size(a) for a in ("lon", "lat", "mem"))
     assert months == devices and sz["highs"] == SUB and lons == 128
-    far = [(de, dl) for dl in range(1, lats) for de in range(members)]
+    far = (lats - 1) * members
 
     def kernel(north_h, up_h, dens_h, thick_h, basin_h, final, *scratch):
         consts, (flux, steps), rest = scratch[:5], scratch[5:7], scratch[7:]
@@ -373,7 +372,6 @@
 
         fixed = pltpu.make_async_copy(basin_h, basin, fix_sem.at[0])
         fixed.start()
-        steps_ahead = min(2, devices * pairs)
         layers(0).start()
         for copy in inputs(0, 0):
             copy.start()
@@ -396,13 +394,13 @@
         zonal = jnp.cos(latitude)
         coef[0] = (north_unit * 0.001) * zonal
         coef[1] = up_unit * zonal
-        flux[:, levels * SUB :, :] = jnp.zeros_like(flux[:, levels * SUB :, :])
+        flux[:, :, levels * SUB :, :] = jnp.zeros_like(flux[:, :, levels * SUB :, :])
         south[...] = jnp.zeros_like(south)
         prepare_weights(sz, consts)
         fixed.wait()
         prepare_masks(sz, basin[...], consts)
-        for i in range(1, steps_ahead):
-            for copy in ([layers(i)] if i < pairs else []) + inputs(i // pairs, i % pairs):
+        for pair in range(1, pairs):
+            for copy in [layers(pair)] + inputs(0, pair):
                 copy.start()
 
         def table_copy(t, pair):
@@ -427,29 +425,8 @@
                 device_id_type=pl.DeviceIdType.MESH,
             )
 
-        hold = min(1, (devices - 1) * pairs - 1)
-
-        def one_pair(i, carry):
-            t, pair = i // pairs, lax.rem(i, pairs)
-
-            @pl.when(i + steps_ahead < devices * pairs)
-            def _():
-                later = i + steps_ahead
-                for copy in inputs(later // pairs, lax.rem(later, pairs)):
-                    copy.start()
-
-            if steps_ahead < pairs:
-
-                @pl.when(i + steps_ahead < pairs)
-                def _():
-                    layers(i + steps_ahead).start()
-
-            @pl.when(t == 0)
-            def _():
-                layers(pair).wait()
-
-            for copy in inputs(t, pair):
-                copy.wait()
+
+        def tables_of(t, pair):
             pair_tables(
                 sz,
                 pair,
@@ -460,23 +437,60 @@
                 coef,
                 consts[0],
                 consts[1],
-                flux,
+                flux.at[pair],
                 tab.at[t, pair],
             )
 
-            @pl.when(i == hold)
+        def one_month(t, carry):
+            @pl.when(t + 1 < devices)
             def _():
-                pl.semaphore_wait(barrier, len(peers))
-                for j in range(hold):
-                    table_copy(j // pairs, j % pairs).start()
-
-            @pl.when((i >= hold) & (t < devices - 1))
+                for pair in range(pairs):
+                    for copy in inputs(t + 1, pair):
+                        copy.start()
+
+            stepwise = (lax.rem(t, 2) == 0) & (t < devices - 1)
+
+            @pl.when(stepwise)
             def _():
-                table_copy(t, pair).start()
+                def one_pair(pair, carry):
+                    @pl.when(t == 0)
+                    def _():
+                        layers(pair).wait()
+
+                    for copy in inputs(t, pair):
+                        copy.wait()
+                    tables_of(t, pair)
+
+                    @pl.when((t == 0) & (pair == pairs - 1))
+                    def _():
+                        pl.semaphore_wait(barrier, len(peers))
+                        for j in range(pairs - 1):
+                            table_copy(t, j).start()
+
+                    @pl.when((t > 0) | (pair == pairs - 1))
+                    def _():
+                        table_copy(t, pair).start()
+
+                    return carry
+
+                lax.fori_loop(0, pairs, one_pair, 0)
+
+            @pl.when(jnp.logical_not(stepwise))
+            def _():
+                for pair in range(pairs):
+                    for copy in inputs(t, pair):
+                        copy.wait()
+                for pair in range(pairs):
+                    tables_of(t, pair)
+
+                @pl.when(t < devices - 1)
+                def _():
+                    for pair in range(pairs):
+                        table_copy(t, pair).start()
 
             return carry
 
-        lax.fori_loop(0, devices * pairs, one_pair, 0)
+        lax.fori_loop(0, devices, one_month, 0)
 
         totals = []
         for pair in range(pairs):
@@ -514,24 +528,30 @@
                 device_id_type=pl.DeviceIdType.MESH,
             )
 
+        def tail_copies(dl):
+            return [tail_copy((dl - 1) * members + de, de, dl) for de in range(members)]
+
         def send_tail(lines):
             for r, line in enumerate(lines):
                 tail[r : r + 1, :] = line
-            for i, (de, dl) in enumerate(far):
+            for dl in range(1, lats):
 
                 @pl.when(lat + dl < lats)
                 def _():
-                    tail_copy(i, de, dl).start()
+                    for copy in tail_copies(dl):
+                        copy.start()
 
         month_sums(sz, totals, consts, steps, mine, send_tail, send_part)
         for s in range(2):
             if s == 1:
-                for i, (de, dl) in enumerate(far):
+                for dl in range(1, lats):
 
                     @pl.when(lat >= dl)
                     def _():
-                        tail_copy(i, de, dl).wait_recv()
-                        south[de] = south[de] + tailbox[i]
+                        for copy in tail_copies(dl):
+                            copy.wait_recv()
+                        for de in range(members):
+                            south[de] = south[de] + tailbox[(dl - 1) * members + de]
 
             for copy in copies[s]:
                 copy.wait_recv()
@@ -558,11 +578,12 @@
                 table_copy(t, pair).wait_send()
         for copy in copies[0] + copies[1]:
             copy.wait_send()
-        for i, (de, dl) in enumerate(far):
+        for dl in range(1, lats):
 
             @pl.when(lat + dl < lats)
             def _():
-                tail_copy(i, de, dl).wait_send()
+                for copy in tail_copies(dl):
+                    copy.wait_send()
 
     arrays = (north_vel, up_vel, dens_class, thickness, basin_id)
     slots = max(1, devices - 1)
@@ -588,7 +609,7 @@
             pltpu.VMEM((2, 2 * lanes, wide), F32),
             pltpu.VMEM((members - 1, 2, 2 * lanes, wide), F32),
             pltpu.VMEM(tails, F32),
-            pltpu.VMEM((len(far),) + tails, F32),
+            pltpu.VMEM((far,) + tails, F32),
             pltpu.VMEM((members,) + tails, F32),
             dma((devices, pairs, 3)),
             dma((1 + pairs,)),
@@ -596,8 +617,8 @@
             dma((slots, pairs)),
             dma((members - 1, 2)),
             dma((members - 1, 2)),
-            dma((len(far),)),
-            dma((len(far),)),
+            dma((far,)),
+            dma((far,)),
         ],
         compiler_params=pltpu.CompilerParams(
             collective_id=0, has_side_effects=True, vmem_limit_bytes=44 * 2**20

time: 20.7 us -> 20.5 us (level)
  the two profiles are of different devices: /device:TPU:21 before, /device:TPU:29 now
where the time goes in v4:
time: 20.5 us; the launch traced here: 20.2 us
  Pallas kernels  19.6 us (96%)
  between operations  0.64 us (3%)
    pallas_call x1, Pallas kernels, fused(): pl.pallas_call(kernel, out_shape=jax.ShapeDtypeStruct((2, tall, wide), F3...  18.8 us
    pallas_call x1, Pallas kernels, place(): pl.pallas_call(kernel, out_shape=[out(levels), out(levels), out(CLASSES),...  0.82 us

profile of v4, /device:TPU:29, one launch (start us, length us, event | category | flops | bytes accessed | tf_op | source)
XLA Modules:
  0.0 20.2 jit_solution(12108277016141574687)
XLA Ops:
  0.6 18.8 %shard_map.84.final = f32[2,512,128]{2,1,0:T(8,128)S(1)} custom-call(bf16[1,4,75,32,128]{4,3,2,1,0:T(8,128)(2,1)} %north_h.1, bf16[1,4,75,32,128]{4,3,2,1,0:T(8,128)(2,1)} %up_h.1, s32[1,4,75,32,128]{4,3,2,1,0:T(8,128)} %dens_h.1, s32[75,32,128]{2,1,0:T(8,128)} %thick_h.1, s32[32,128]{1,0:T(8,128)} %basin_h.1), custom_call_target="tpu_custom_call" | custom-call | tf_op jit(solution)/shard_map/pallas_call | solution.py:593
  19.4 0.8 %shard_map.85 = (f32[1,4,2,32,75]{4,3,2,1,0:T(8,128)}, f32[1,4,2,32,75]{4,3,2,1,0:T(8,128)}, f32[1,4,2,32,80]{4,3,2,1,0:T(8,128)}, f32[1,4,2,32,80]{4,3,2,1,0:T(8,128)}) custom-call(f32[2,512,128]{2,1,0:T(8,128)S(1)} %shard_map.84.final), custom_call_target="tpu_custom_call" | custom-call | tf_op jit(solution)/shard_map/pallas_call | solution.py:642

commit v5 on v4

--- a/solution.py
+++ b/solution.py
@@ -233,20 +233,24 @@
     return slice(at, at + sz["lanes"])
 
 
-def month_sums(sz, total, consts, steps, mine, send_tail, send_part):
+def month_sums(sz, total_of, consts, steps, mine, send_tail, send_part):
     _, _, upto_class, upto_level, upto_row = consts
     rows, pairs, highs, span = sz["rows"], sz["pairs"], sz["highs"], sz["span"]
     width, wide = LOW * SUB, sz["wide"]
     row, lane = iota((SUB, 128), 0), iota((SUB, 128), 1)
     own = row == lane % SUB
+    deep = []
     for pair in range(pairs):
+        total = total_of(pair)
+        x = total[class_row(2, 0, 0) :]
+        deep.append(jnp.concatenate([x, jnp.zeros((wide - x.shape[0], 128), F32)], 0).T)
         for s in range(2):
             exact = []
             for half in range(2):
                 here, back = [], []
                 for c in range(width // 128):
                     at = class_row(half, s, c)
-                    x = total[pair][at : at + SUB]
+                    x = total[at : at + SUB]
                     x = x - jnp.where(row < highs - 1, pltpu.roll(x, SUB - 1, 0), 0.0)
                     here.append(x)
                     back.append(pltpu.roll(x, 2 * SUB, 1))
@@ -276,10 +280,6 @@
         x = lax.dot_general(steps[:, cols], upto_class[b], NN, preferred_element_type=F32)
         found.append(x[: 2 * rows] + x[2 * rows :])
     found = [sum(found[1:], found[0])] + found
-    deep = []
-    for pair in range(pairs):
-        x = total[pair][class_row(2, 0, 0) :]
-        deep.append(jnp.concatenate([x, jnp.zeros((wide - x.shape[0], 128), F32)], 0).T)
     tables = []
     for s in range(2):
         classes = jnp.concatenate([x[s * rows : (s + 1) * rows] for x in found], 0)
@@ -492,13 +492,13 @@
 
         lax.fori_loop(0, devices, one_month, 0)
 
-        totals = []
-        for pair in range(pairs):
+        def total_of(pair):
             total = tab[devices - 1, pair]
             for t in range(devices - 1):
                 arrival(t, pair).wait_recv()
                 total = total + inbox[t, pair]
-            totals.append(total)
+            return total
+
         copies = [
             [
                 pltpu.make_async_remote_copy(
@@ -541,7 +541,7 @@
                     for copy in tail_copies(dl):
                         copy.start()
 
-        month_sums(sz, totals, consts, steps, mine, send_tail, send_part)
+        month_sums(sz, total_of, consts, steps, mine, send_tail, send_part)
         for s in range(2):
             if s == 1:
                 for dl in range(1, lats):

time: 20.5 us -> 20.4 us (level)
  the two profiles are of different devices: /device:TPU:29 before, /device:TPU:21 now
where the time goes in v5:
time: 20.4 us; the launch traced here: 20.2 us
  Pallas kernels  19.6 us (96%)
  between operations  0.64 us (3%)
    pallas_call x1, Pallas kernels, fused(): pl.pallas_call(kernel, out_shape=jax.ShapeDtypeStruct((2, tall, wide), F3...  18.7 us
    pallas_call x1, Pallas kernels, place(): pl.pallas_call(kernel, out_shape=[out(levels), out(levels), out(CLASSES),...  0.82 us

profile of v5, /device:TPU:21, one launch (start us, length us, event | category | flops | bytes accessed | tf_op | source)
XLA Modules:
  0.0 20.2 jit_solution(12893954267651360712)
XLA Ops:
  0.6 18.7 %shard_map.84.final = f32[2,512,128]{2,1,0:T(8,128)S(1)} custom-call(bf16[1,4,75,32,128]{4,3,2,1,0:T(8,128)(2,1)} %north_h.1, bf16[1,4,75,32,128]{4,3,2,1,0:T(8,128)(2,1)} %up_h.1, s32[1,4,75,32,128]{4,3,2,1,0:T(8,128)} %dens_h.1, s32[75,32,128]{2,1,0:T(8,128)} %thick_h.1, s32[32,128]{1,0:T(8,128)} %basin_h.1), custom_call_target="tpu_custom_call" | custom-call | tf_op jit(solution)/shard_map/pallas_call | solution.py:593
  19.4 0.8 %shard_map.85 = (f32[1,4,2,32,75]{4,3,2,1,0:T(8,128)}, f32[1,4,2,32,75]{4,3,2,1,0:T(8,128)}, f32[1,4,2,32,80]{4,3,2,1,0:T(8,128)}, f32[1,4,2,32,80]{4,3,2,1,0:T(8,128)}) custom-call(f32[2,512,128]{2,1,0:T(8,128)S(1)} %shard_map.84.final), custom_call_target="tpu_custom_call" | custom-call | tf_op jit(solution)/shard_map/pallas_call | solution.py:642
